TPU v7x, 32 devices: a whole 2x2x4 slice. The times are simulated.
32 devices in a mesh: gz: 2 (over x), gy: 4 (over y, core), gx: 4 (over z).
Axes of the slice: x: 2, y: 2, z: 4, core: 2. Of those that a mesh axis runs over, the one named last changes fastest.
Arguments:
- density: float32 [32, 64, 256], P('gx', 'gy', 'gz'), may hold values from 0.05 to 0.95
- spread: float32 [32, 64, 256], P('gx', 'gy', 'gz'), may hold values from 0.05 to 0.3
- sensitivities: float32 [9, 32, 64, 256], P(None, 'gx', 'gy', 'gz'), may hold values from -180 to 180, as said below
- violation: float32 [9], replicated, may hold values from -0.05 to 0.15
- multipliers_start: float32 [9], replicated, may hold values from 0.1 to 10
Outputs:
- new_density: float32 [32, 64, 256], P('gx', 'gy', 'gz')
- multipliers: float32 [9], replicated
Inputs may be any that keep to these rules, and one draw needn't show every extreme that they name: `sensitivities`: Real-valued, independent from voxel to voxel.
All inputs are finite; a program needn't handle non-finite values.
Results may differ from a plain program's by a relative error of at most 0.0003.
Values sent between devices are 32-bit elements; how exact they have to be, the bound alone decides.
A program may use at most 64 MiB of HBM per device.

v0:
```python
import math
import jax
import jax.numpy as jnp
from jax import lax
from jax.sharding import PartitionSpec as P

FIELDS = 9
ITERS = 3
RADIUS = 3.0
RAA = 1e-05
MOVE = 0.9
REG = 0.001
FLOOR = 0.2


def padded_2(block, sides, width):
    for axis, dim in sides:
        count = lax.axis_size(axis)
        forward = [(i, i + 1) for i in range(count - 1)]
        backward = [(target, source) for source, target in forward]
        low = lax.ppermute(
            lax.slice_in_dim(block, block.shape[dim] - width, None, axis=dim), axis, forward
        )
        high = lax.ppermute(lax.slice_in_dim(block, 0, width, axis=dim), axis, backward)
        block = jnp.concatenate([low, block, high], axis=dim)
    return block


def smooth(padded, nx, ny, nz):
    total = None
    for a in (-1, 0, 1):
        for b in (-1, 0, 1):
            for c in (-1, 0, 1):
                weight = RADIUS - math.sqrt(a * a + b * b + c * c)
                piece = padded[..., 1 + a : 1 + a + nx, 1 + b : 1 + b + ny, 1 + c : 1 + c + nz]
                total = weight * piece if total is None else total + weight * piece
    return total


def inside(index, extent, count):
    first = (index > 0).astype(jnp.float32)
    last = (index < extent - 1).astype(jnp.float32)
    return jnp.concatenate([first[None], jnp.ones((count,), jnp.float32), last[None]])


def totals(gradient_part, schur_part):
    return lax.psum((gradient_part, schur_part), ("gz", "gy", "gx"))


def shards(density, spread, sensitivities, violation, multipliers_start):
    nx, ny, nz = density.shape
    padded = padded_2(sensitivities, (("gz", 3), ("gy", 2), ("gx", 1)), 1)
    mask_x = inside(lax.axis_index("gx"), lax.axis_size("gx"), nx)
    mask_y = inside(lax.axis_index("gy"), lax.axis_size("gy"), ny)
    mask_z = inside(lax.axis_index("gz"), lax.axis_size("gz"), nz)
    valid = mask_x[:, None, None] * mask_y[None, :, None] * mask_z[None, None, :]
    denom = smooth(valid, nx, ny, nz)
    filtered = smooth(padded, nx, ny, nz) / denom[None]
    cells = nx * ny * nz
    dens = density.reshape(-1)
    span = spread.reshape(-1)
    rows = jnp.concatenate(
        [filtered.reshape(FIELDS, cells), jnp.ones((1, cells), jnp.float32)], axis=0
    )
    grow = jnp.maximum(rows, 0.0)
    fall = jnp.maximum(-rows, 0.0)
    square = span * span
    pp = square * (1.001 * grow + 0.001 * fall + RAA)
    qq = square * (0.001 * grow + 1.001 * fall + RAA)
    lower = dens - span
    upper = dens + span
    floor_x = jnp.maximum(0.0, dens - MOVE * span)
    ceil_x = jnp.minimum(1.0, dens + MOVE * span)
    base = (pp[1:] + qq[1:]) / span
    keep = 1.0 - violation
    base_local = jnp.sum(base, axis=1)
    bound = None
    bound = keep * lax.psum(base_local, ("gz", "gy", "gx"))

    def respond(lam):
        weights = jnp.concatenate([jnp.ones((1,), jnp.float32), lam])
        big_p = jnp.dot(weights, pp, precision=lax.Precision.HIGHEST)
        big_q = jnp.dot(weights, qq, precision=lax.Precision.HIGHEST)
        root_p = jnp.sqrt(big_p)
        root_q = jnp.sqrt(big_q)
        moved = (root_p * lower + root_q * upper) / (root_p + root_q)
        return (jnp.clip(moved, floor_x, ceil_x), big_p, big_q)

    lam = multipliers_start
    for step in range(ITERS):
        moved, big_p, big_q = respond(lam)
        above = upper - moved
        below = moved - lower
        values = pp[1:] / above + qq[1:] / below
        slopes = pp[1:] / (above * above) - qq[1:] / (below * below)
        curv = 2.0 * big_p / (above * above * above) + 2.0 * big_q / (below * below * below)
        schur_part = jnp.dot(slopes / curv, slopes.T, precision=lax.Precision.HIGHEST)
        summed, schur = totals(jnp.sum(values, axis=1), schur_part)
        gradient = summed - bound
        shift = REG * jnp.trace(schur) / FIELDS
        system = schur + shift * jnp.eye(FIELDS, dtype=jnp.float32)
        factor = jnp.linalg.cholesky(system)
        delta = jax.scipy.linalg.cho_solve((factor, True), gradient)
        lam = jnp.maximum(lam + delta, FLOOR * lam)
    moved, big_p, big_q = respond(lam)
    return (moved.reshape(nx, ny, nz), lam)


def solution(mesh):
    return jax.shard_map(
        shards,
        mesh=mesh,
        in_specs=(P("gx", "gy", "gz"), P("gx", "gy", "gz"), P(None, "gx", "gy", "gz"), P(), P()),
        out_specs=(P("gx", "gy", "gz"), P()),
        check_vma=False,
    )
```

profile of v0, /device:TPU:0, one launch (start us, length us, event | category | flops | bytes accessed | tf_op | source)
XLA Modules:
  0.0 187.6 jit_solution(5219307162577140861)
XLA Ops:
  0.6 1.5 fusion.136
  2.7 4.9 %collective-permute-start = (f32[9,8,16,1]{2,1,3,0:T(8,128)S(1)}, f32[9,8,16,1]{2,1,3,0:T(8,128)S(1)}, u32[]{:S(2)}, u32[]{:S(2)}) collective-permute-start(f32[9,8,16,1]{2,1,3,0:T(8,128)S(1)} %copy.82), channel_id=1, source_target_pairs={{0,16},{1,17},{2,18},{3,19},{4,20},{5,21},{6,22},{7,23},{8,24},{9,... | collective-permute-start | bytes 13832 | tf_op jit(solution)/shard_map/ppermute | solution.py:21
  8.0 1.3 collective-permute-start.1
  10.5 3.4 %collective-permute-done.1 = f32[9,8,16,1]{2,1,3,0:T(8,128)S(1)} collective-permute-done((f32[9,8,16,1]{2,1,3,0:T(8,128)S(1)}, f32[9,8,16,1]{2,1,3,0:T(8,128)S(1)}, u32[]{:S(2)}, u32[]{:S(2)}) %collective-permute-start.1) | collective-permute-done | bytes 4640 | tf_op jit(solution)/shard_map/ppermute | solution.py:24
  14.5 1.3 collective-permute-start.2
  15.8 1.3 collective-permute-start.3
  17.5 3.2 %collective-permute-done.3 = f32[9,8,1,130]{3,1,2,0:T(8,128)S(1)} collective-permute-done((f32[9,8,1,130]{3,1,2,0:T(8,128)S(1)}, f32[9,8,1,130]{3,1,2,0:T(8,128)S(1)}, u32[]{:S(2)}, u32[]{:S(2)}) %collective-permute-start.3) | collective-permute-done | bytes 37472 | tf_op jit(solution)/shard_map/ppermute | solution.py:24
  20.7 1.0 pad_maximum_fusion.8
  21.7 3.5 %collective-permute-start.4 = (f32[9,1,18,130]{3,2,1,0:T(8,128)S(1)}, f32[9,1,18,130]{3,2,1,0:T(8,128)S(1)}, u32[]{:S(2)}, u32[]{:S(2)}) collective-permute-start(f32[9,1,18,130]{3,2,1,0:T(8,128)S(1)} %copy.60), channel_id=1, source_target_pairs={{0,1},{1,2},{2,3},{4,5},{5,6},{6,7},{8,9},{9,10},{10,11},{12,13},{... | collective-permute-start | bytes 252728 | tf_op jit(solution)/shard_map/ppermute | solution.py:21
  25.3 1.5 collective-permute-start.5
  26.7 1.0 maximum_maximum_fusion.1
  27.7 1.3 collective-permute-done.4
  29.2 4.5 %collective-permute-done.5 = f32[9,1,18,130]{3,2,1,0:T(8,128)S(1)} collective-permute-done((f32[9,1,18,130]{3,2,1,0:T(8,128)S(1)}, f32[9,1,18,130]{3,2,1,0:T(8,128)S(1)}, u32[]{:S(2)}, u32[]{:S(2)}) %collective-permute-start.5) | collective-permute-done | bytes 84272 | tf_op jit(solution)/shard_map/ppermute | solution.py:24
  33.9 2.1 %maximum_maximum_fusion = (f32[9,9,18,130]{3,1,2,0:T(8,128)S(1)}, f32[9,9,18,130]{3,1,2,0:T(8,128)S(1)}) fusion(f32[9,8,1,130]{3,1,2,0:T(8,128)S(1)} %collective-permute-done.3, f32[9,8,16,1]{3,1,2,0:T(8,128)S(1)} %copy.59, f32[9,8,16,128]{3,1,2,0:T(8,128)S(1)} %copy.58, f32[9,8,16,1]{3,1,2,0:T(8,128)S(1)} %copy.57, ...), kind=kLoop, calls=%fused_computation | loop fusion | flops 1895400 | bytes 2358720 | tf_op jit(solution)/shard_map/concatenate | solution.py:25
  36.0 3.1 %fusion.29 = f32[9,8,16,128]{3,1,2,0:T(8,128)S(1)} fusion(f32[9,9,18,130]{3,1,2,0:T(8,128)S(1)} %get-tuple-element.33, f32[9,8,17,130]{3,1,2,0:T(8,128)S(1)} %get-tuple-element.37, f32[9,8,16,1]{3,1,2,0:T(8,128)S(1)} %copy.59, f32[9,8,16,128]{3,1,2,0:T(8,128)S(1)} %copy.58, f32[9,8,16,1]{3,1,2,0:T(8,128)S(1)} %copy.57, ...), kind=kLoop, calls=%fused_computation.47 | loop fusion | flops 8257536 | bytes 15410176 | tf_op jit(solution)/shard_map/div | solution.py:58
  41.9 0.8 fusion.21
  42.8 1.7 fusion.4
  44.5 40.1 %all-reduce.3 = (f32[9,9]{0,1:T(8,128)S(1)}, f32[9]{0:T(128)S(1)}, f32[9]{0:T(128)S(1)}) all-reduce(f32[9,9]{0,1:T(8,128)S(1)} %fusion.4, f32[9]{0:T(128)S(1)} %get-tuple-element.5, f32[9]{0:T(128)S(1)} %get-tuple-element.4), channel_id=1, replica_groups=mesh['gz'=2,'gy'=4,'gx'=4] {'gz','gy','gx'}, use_global_device_ids=true, to_apply=%region_0.0 | all-reduce | flops 99 | bytes 792 | tf_op jit(solution)/shard_map/psum | solution.py:47
  86.0 0.8 cholesky.59
  91.0 1.7 fusion.2
  92.7 40.2 %all-reduce.2 = (f32[9,9]{0,1:T(8,128)S(1)}, f32[9]{0:T(128)S(1)}) all-reduce(f32[9,9]{0,1:T(8,128)S(1)} %fusion.2, f32[9]{0:T(128)S(1)} %add_reduce_fusion.1), channel_id=1, replica_groups=mesh['gz'=2,'gy'=4,'gx'=4] {'gz','gy','gx'}, use_global_device_ids=true, to_apply=%region_8.11 | all-reduce | flops 90 | bytes 720 | tf_op jit(solution)/shard_map/psum | solution.py:47
  134.2 0.8 cholesky.70
  139.3 1.7 fusion
  140.9 40.1 %all-reduce.1 = (f32[9,9]{0,1:T(8,128)S(1)}, f32[9]{0:T(128)S(1)}) all-reduce(f32[9,9]{0,1:T(8,128)S(1)} %fusion, f32[9]{0:T(128)S(1)} %add_reduce_fusion), channel_id=1, replica_groups=mesh['gz'=2,'gy'=4,'gx'=4] {'gz','gy','gx'}, use_global_device_ids=true, to_apply=%region_12.15 | all-reduce | flops 90 | bytes 720 | tf_op jit(solution)/shard_map/psum | solution.py:47
  (89 shorter events, 21.8 us)
Async XLA Ops:
  0.6 9.2 %copy-start = (f32[9,8,16,128]{3,2,1,0:T(8,128)S(1)}, f32[9,8,16,128]{3,2,1,0:T(8,128)}, u32[]{:S(2)}) copy-start(f32[9,8,16,128]{3,2,1,0:T(8,128)} %param.10) | copy-start | bytes 1769476
  2.7 7.4 %collective-permute-start = (f32[9,8,16,1]{2,1,3,0:T(8,128)S(1)}, f32[9,8,16,1]{2,1,3,0:T(8,128)S(1)}, u32[]{:S(2)}, u32[]{:S(2)}) collective-permute-start(f32[9,8,16,1]{2,1,3,0:T(8,128)S(1)} %copy.82), channel_id=1, source_target_pairs={{0,16},{1,17},{2,18},{3,19},{4,20},{5,21},{6,22},{7,23},{8,24},{9,... | collective-permute-start | bytes 13832 | tf_op jit(solution)/shard_map/ppermute | solution.py:21
  8.0 5.9 %collective-permute-start.1 = (f32[9,8,16,1]{2,1,3,0:T(8,128)S(1)}, f32[9,8,16,1]{2,1,3,0:T(8,128)S(1)}, u32[]{:S(2)}, u32[]{:S(2)}) collective-permute-start(f32[9,8,16,1]{2,1,3,0:T(8,128)S(1)} %copy.83), channel_id=1, source_target_pairs={{16,0},{17,1},{18,2},{19,3},{20,4},{21,5},{22,6},{23,7},{24,8},{25... | collective-permute-start | bytes 13832 | tf_op jit(solution)/shard_map/ppermute | solution.py:24
  10.0 7.5 %copy-start.1 = (f32[8,16,128]{2,1,0:T(8,128)S(1)}, f32[8,16,128]{2,1,0:T(8,128)}, u32[]{:S(2)}) copy-start(f32[8,16,128]{2,1,0:T(8,128)} %param.9) | copy-start | bytes 196612
  14.5 3.0 %collective-permute-start.2 = (f32[9,8,1,130]{3,1,2,0:T(8,128)S(1)}, f32[9,8,1,130]{3,1,2,0:T(8,128)S(1)}, u32[]{:S(2)}, u32[]{:S(2)}) collective-permute-start(f32[9,8,1,130]{3,1,2,0:T(8,128)S(1)} %get-tuple-element.38), channel_id=1, source_target_pairs={{0,4},{4,8},{8,12},{1,5},{5,9},{9,13},{2,6},{6,10},{10,14},{3,7},{... | collective-permute-start | bytes 112328 | tf_op jit(solution)/shard_map/ppermute | solution.py:21
  15.8 4.9 %collective-permute-start.3 = (f32[9,8,1,130]{3,1,2,0:T(8,128)S(1)}, f32[9,8,1,130]{3,1,2,0:T(8,128)S(1)}, u32[]{:S(2)}, u32[]{:S(2)}) collective-permute-start(f32[9,8,1,130]{3,1,2,0:T(8,128)S(1)} %get-tuple-element.39), channel_id=1, source_target_pairs={{4,0},{8,4},{12,8},{5,1},{9,5},{13,9},{6,2},{10,6},{14,10},{7,3},{... | collective-permute-start | bytes 112328 | tf_op jit(solution)/shard_map/ppermute | solution.py:24
  21.7 7.3 %collective-permute-start.4 = (f32[9,1,18,130]{3,2,1,0:T(8,128)S(1)}, f32[9,1,18,130]{3,2,1,0:T(8,128)S(1)}, u32[]{:S(2)}, u32[]{:S(2)}) collective-permute-start(f32[9,1,18,130]{3,2,1,0:T(8,128)S(1)} %copy.60), channel_id=1, source_target_pairs={{0,1},{1,2},{2,3},{4,5},{5,6},{6,7},{8,9},{9,10},{10,11},{12,13},{... | collective-permute-start | bytes 252728 | tf_op jit(solution)/shard_map/ppermute | solution.py:21
  25.3 8.4 %collective-permute-start.5 = (f32[9,1,18,130]{3,2,1,0:T(8,128)S(1)}, f32[9,1,18,130]{3,2,1,0:T(8,128)S(1)}, u32[]{:S(2)}, u32[]{:S(2)}) collective-permute-start(f32[9,1,18,130]{3,2,1,0:T(8,128)S(1)} %copy.67), channel_id=1, source_target_pairs={{1,0},{2,1},{3,2},{5,4},{6,5},{7,6},{9,8},{10,9},{11,10},{13,12},{... | collective-permute-start | bytes 252728 | tf_op jit(solution)/shard_map/ppermute | solution.py:24
  39.3 1.2 copy-start.3
  40.0 1.8 copy-start.2
  42.8 46.0 %copy-start.5 = (f32[9]{0:T(128)S(1)}, f32[9]{0:T(128)}, u32[]{:S(2)}) copy-start(f32[9]{0:T(128)} %param.11) | copy-start | bytes 112
  185.6 2.0 %copy-start.4 = (f32[9]{0:T(128)}, f32[9]{0:T(128)S(1)}, u32[]{:S(2)}) copy-start(f32[9]{0:T(128)S(1)} %fusion.11) | copy-start | bytes 112
where the time goes:
time: 188 us
  blocking collectives  120 us (64%)
  other arithmetic  21.8 us (12%)
  starting transfers between devices  13.7 us (7%)
  waiting for transfers between devices  12.4 us (7%)
  matrix products  11 us (6%)
  local copies, waits for them, and re-layouts  5.18 us (3%)
  between operations  3.06 us (2%)
    psum x3, blocking collectives, totals(): return lax.psum((gradient_part, schur_part), ('gz', 'gy', 'gx'))  120 us
    ppermute x3, waiting for transfers between devices, padded_2(): lax.ppermute(lax.slice_in_dim(block, 0, width, axis=dim), axis, backward)  11.1 us
    ppermute x3, starting transfers between devices, padded_2(): lax.ppermute(lax.slice_in_dim(block, block.shape[dim] - width, None, axis...  9.67 us
    dot_general x3, matrix products, shards(): jnp.dot(slopes / curv, slopes.T, precision=lax.Precision.HIGHEST)  5.02 us
    another operation x9, other arithmetic, shards(): factor = jnp.linalg.cholesky(system)  4.45 us
    ppermute x3, starting transfers between devices, padded_2(): lax.ppermute(lax.slice_in_dim(block, 0, width, axis=dim), axis, backward)  4.06 us
    another operation x6, other arithmetic, shards(): delta = jax.scipy.linalg.cho_solve((factor, True), gradient)  4.03 us
  transfers between devices with their start and end apart: 6, of which 4 were waited for; matrix products, arithmetic and copies ran while one was open for 2% of the time, Pallas kernels for 0%

commit v1 on v0

--- a/solution.py
+++ b/solution.py
@@ -44,7 +44,7 @@
 
 
 def totals(gradient_part, schur_part):
-    return lax.psum((gradient_part, schur_part), ("gz", "gy", "gx"))
+    return lax.psum(lax.psum((gradient_part, schur_part), ("gy", "gx")), "gz")
 
 
 def shards(density, spread, sensitivities, violation, multipliers_start):

time: 188 us -> 219 us (1.16)
  blocking collectives: 120 us -> 152 us
    psum x3 -> x7, blocking collectives: 120 us -> 152 us  [the longest x6 113 us: totals(): return lax.psum(lax.psum((gradient_part, schur_part), ('gy', 'gx')), 'gz')]
  transfers between devices with their start and end apart: 6 -> 6, of which waited for: 4 -> 4; matrix products, arithmetic and copies ran while one was open for 2% -> 1% of each run, Pallas kernels for 0% -> 0%
where the time goes in v1:
time: 219 us
  blocking collectives  152 us (69%)
  other arithmetic  21.8 us (10%)
  starting transfers between devices  13.7 us (6%)
  waiting for transfers between devices  12.4 us (6%)
  matrix products  11 us (5%)
  local copies, waits for them, and re-layouts  5.18 us (2%)
  between operations  3.08 us (1%)
    psum x6, blocking collectives, totals(): return lax.psum(lax.psum((gradient_part, schur_part), ('gy', 'gx')), 'gz')  113 us
    psum x1, blocking collectives, shards(): bound = keep * lax.psum(base_local, ('gz', 'gy', 'gx'))  38.9 us
    ppermute x3, waiting for transfers between devices, padded_2(): lax.ppermute(lax.slice_in_dim(block, 0, width, axis=dim), axis, backward)  11.1 us
    ppermute x3, starting transfers between devices, padded_2(): lax.ppermute(lax.slice_in_dim(block, block.shape[dim] - width, None, axis...  9.67 us
    dot_general x3, matrix products, shards(): jnp.dot(slopes / curv, slopes.T, precision=lax.Precision.HIGHEST)  5.02 us
    another operation x9, other arithmetic, shards(): factor = jnp.linalg.cholesky(system)  4.45 us
  transfers between devices with their start and end apart: 6, of which 4 were waited for; matrix products, arithmetic and copies ran while one was open for 1% of the time, Pallas kernels for 0%

profile of v1, /device:TPU:0, one launch (start us, length us, event | category | flops | bytes accessed | tf_op | source)
XLA Modules:
  0.0 218.8 jit_solution(12521374528929716191)
XLA Ops:
  0.6 1.5 fusion.136
  2.7 4.9 %collective-permute-start = (f32[9,8,16,1]{2,1,3,0:T(8,128)S(1)}, f32[9,8,16,1]{2,1,3,0:T(8,128)S(1)}, u32[]{:S(2)}, u32[]{:S(2)}) collective-permute-start(f32[9,8,16,1]{2,1,3,0:T(8,128)S(1)} %copy.82), channel_id=1, source_target_pairs={{0,16},{1,17},{2,18},{3,19},{4,20},{5,21},{6,22},{7,23},{8,24},{9,... | collective-permute-start | bytes 13832 | tf_op jit(solution)/shard_map/ppermute | solution.py:21
  8.0 1.3 collective-permute-start.1
  10.5 3.4 %collective-permute-done.1 = f32[9,8,16,1]{2,1,3,0:T(8,128)S(1)} collective-permute-done((f32[9,8,16,1]{2,1,3,0:T(8,128)S(1)}, f32[9,8,16,1]{2,1,3,0:T(8,128)S(1)}, u32[]{:S(2)}, u32[]{:S(2)}) %collective-permute-start.1) | collective-permute-done | bytes 4640 | tf_op jit(solution)/shard_map/ppermute | solution.py:24
  14.5 1.3 collective-permute-start.2
  15.8 1.3 collective-permute-start.3
  17.5 3.2 %collective-permute-done.3 = f32[9,8,1,130]{3,1,2,0:T(8,128)S(1)} collective-permute-done((f32[9,8,1,130]{3,1,2,0:T(8,128)S(1)}, f32[9,8,1,130]{3,1,2,0:T(8,128)S(1)}, u32[]{:S(2)}, u32[]{:S(2)}) %collective-permute-start.3) | collective-permute-done | bytes 37472 | tf_op jit(solution)/shard_map/ppermute | solution.py:24
  21.7 3.5 %collective-permute-start.4 = (f32[9,1,18,130]{3,2,1,0:T(8,128)S(1)}, f32[9,1,18,130]{3,2,1,0:T(8,128)S(1)}, u32[]{:S(2)}, u32[]{:S(2)}) collective-permute-start(f32[9,1,18,130]{3,2,1,0:T(8,128)S(1)} %copy.60), channel_id=1, source_target_pairs={{0,1},{1,2},{2,3},{4,5},{5,6},{6,7},{8,9},{9,10},{10,11},{12,13},{... | collective-permute-start | bytes 252728 | tf_op jit(solution)/shard_map/ppermute | solution.py:21
  25.3 1.5 collective-permute-start.5
  26.7 1.0 maximum_maximum_fusion.1
  27.7 1.3 collective-permute-done.4
  29.2 4.5 %collective-permute-done.5 = f32[9,1,18,130]{3,2,1,0:T(8,128)S(1)} collective-permute-done((f32[9,1,18,130]{3,2,1,0:T(8,128)S(1)}, f32[9,1,18,130]{3,2,1,0:T(8,128)S(1)}, u32[]{:S(2)}, u32[]{:S(2)}) %collective-permute-start.5) | collective-permute-done | bytes 84272 | tf_op jit(solution)/shard_map/ppermute | solution.py:24
  33.9 2.1 maximum_maximum_fusion
  36.0 3.1 %fusion.29 = f32[9,8,16,128]{3,1,2,0:T(8,128)S(1)} fusion(f32[9,9,18,130]{3,1,2,0:T(8,128)S(1)} %get-tuple-element.38, f32[9,8,17,130]{3,1,2,0:T(8,128)S(1)} %get-tuple-element.42, f32[9,8,16,1]{3,1,2,0:T(8,128)S(1)} %copy.59, f32[9,8,16,128]{3,1,2,0:T(8,128)S(1)} %copy.58, f32[9,8,16,1]{3,1,2,0:T(8,128)S(1)} %copy.57, ...), kind=kLoop, calls=%fused_computation.47 | loop fusion | flops 8257536 | bytes 15410176 | tf_op jit(solution)/shard_map/div | solution.py:58
  42.8 1.7 fusion.4
  44.5 32.7 %all-reduce.3 = (f32[9,9]{0,1:T(8,128)S(1)}, f32[9]{0:T(128)S(1)}) all-reduce(f32[9,9]{0,1:T(8,128)S(1)} %fusion.4, f32[9]{0:T(128)S(1)} %get-tuple-element.5), channel_id=1, replica_groups=mesh['gz'=2,'gy'=4,'gx'=4] {'gy','gx'}, use_global_device_ids=true, to_apply=%region_0.0 | all-reduce | flops 90 | bytes 720 | tf_op jit(solution)/shard_map/psum | solution.py:47
  77.2 5.1 %all-reduce.6 = (f32[9,9]{0,1:T(8,128)S(1)}, f32[9]{0:T(128)S(1)}) all-reduce(f32[9,9]{0,1:T(8,128)S(1)} %get-tuple-element.10, f32[9]{0:T(128)S(1)} %get-tuple-element.11), channel_id=1, replica_groups=mesh['gz'=2,'gy'=4,'gx'=4] {'gz'}, use_global_device_ids=true, to_apply=%region_1.0 | all-reduce | flops 90 | bytes 720 | tf_op jit(solution)/shard_map/psum | solution.py:47
  86.5 38.9 %psum.95 = f32[9]{0:T(128)S(1)} all-reduce(f32[9]{0:T(128)S(1)} %get-tuple-element.4), channel_id=1, replica_groups=mesh['gz'=2,'gy'=4,'gx'=4] {'gz','gy','gx'}, use_global_device_ids=true, to_apply=%region_9.11 | all-reduce | flops 9 | bytes 72 | tf_op jit(solution)/shard_map/psum | solution.py:78
  127.6 1.7 fusion.2
  129.3 33.7 %all-reduce.2 = (f32[9,9]{0,1:T(8,128)S(1)}, f32[9]{0:T(128)S(1)}) all-reduce(f32[9,9]{0,1:T(8,128)S(1)} %fusion.2, f32[9]{0:T(128)S(1)} %add_reduce_fusion.1), channel_id=1, replica_groups=mesh['gz'=2,'gy'=4,'gx'=4] {'gy','gx'}, use_global_device_ids=true, to_apply=%region_10.13 | all-reduce | flops 90 | bytes 720 | tf_op jit(solution)/shard_map/psum | solution.py:47
  163.0 5.1 %all-reduce.5 = (f32[9,9]{0,1:T(8,128)S(1)}, f32[9]{0:T(128)S(1)}) all-reduce(f32[9,9]{0,1:T(8,128)S(1)} %get-tuple-element.8, f32[9]{0:T(128)S(1)} %get-tuple-element.9), channel_id=1, replica_groups=mesh['gz'=2,'gy'=4,'gx'=4] {'gz'}, use_global_device_ids=true, to_apply=%region_11.14 | all-reduce | flops 90 | bytes 720 | tf_op jit(solution)/shard_map/psum | solution.py:47
  174.5 1.7 fusion
  176.1 31.1 %all-reduce.1 = (f32[9,9]{0,1:T(8,128)S(1)}, f32[9]{0:T(128)S(1)}) all-reduce(f32[9,9]{0,1:T(8,128)S(1)} %fusion, f32[9]{0:T(128)S(1)} %add_reduce_fusion), channel_id=1, replica_groups=mesh['gz'=2,'gy'=4,'gx'=4] {'gy','gx'}, use_global_device_ids=true, to_apply=%region_16.19 | all-reduce | flops 90 | bytes 720 | tf_op jit(solution)/shard_map/psum | solution.py:47
  207.2 5.1 %all-reduce.4 = (f32[9,9]{0,1:T(8,128)S(1)}, f32[9]{0:T(128)S(1)}) all-reduce(f32[9,9]{0,1:T(8,128)S(1)} %get-tuple-element.6, f32[9]{0:T(128)S(1)} %get-tuple-element.7), channel_id=1, replica_groups=mesh['gz'=2,'gy'=4,'gx'=4] {'gz'}, use_global_device_ids=true, to_apply=%region_17.20 | all-reduce | flops 90 | bytes 720 | tf_op jit(solution)/shard_map/psum | solution.py:47
  (93 shorter events, 25.2 us)
Async XLA Ops:
  0.6 9.2 %copy-start = (f32[9,8,16,128]{3,2,1,0:T(8,128)S(1)}, f32[9,8,16,128]{3,2,1,0:T(8,128)}, u32[]{:S(2)}) copy-start(f32[9,8,16,128]{3,2,1,0:T(8,128)} %param.10) | copy-start | bytes 1769476
  2.7 7.4 %collective-permute-start = (f32[9,8,16,1]{2,1,3,0:T(8,128)S(1)}, f32[9,8,16,1]{2,1,3,0:T(8,128)S(1)}, u32[]{:S(2)}, u32[]{:S(2)}) collective-permute-start(f32[9,8,16,1]{2,1,3,0:T(8,128)S(1)} %copy.82), channel_id=1, source_target_pairs={{0,16},{1,17},{2,18},{3,19},{4,20},{5,21},{6,22},{7,23},{8,24},{9,... | collective-permute-start | bytes 13832 | tf_op jit(solution)/shard_map/ppermute | solution.py:21
  8.0 5.9 %collective-permute-start.1 = (f32[9,8,16,1]{2,1,3,0:T(8,128)S(1)}, f32[9,8,16,1]{2,1,3,0:T(8,128)S(1)}, u32[]{:S(2)}, u32[]{:S(2)}) collective-permute-start(f32[9,8,16,1]{2,1,3,0:T(8,128)S(1)} %copy.83), channel_id=1, source_target_pairs={{16,0},{17,1},{18,2},{19,3},{20,4},{21,5},{22,6},{23,7},{24,8},{25... | collective-permute-start | bytes 13832 | tf_op jit(solution)/shard_map/ppermute | solution.py:24
  10.0 7.5 %copy-start.1 = (f32[8,16,128]{2,1,0:T(8,128)S(1)}, f32[8,16,128]{2,1,0:T(8,128)}, u32[]{:S(2)}) copy-start(f32[8,16,128]{2,1,0:T(8,128)} %param.9) | copy-start | bytes 196612
  14.5 3.0 %collective-permute-start.2 = (f32[9,8,1,130]{3,1,2,0:T(8,128)S(1)}, f32[9,8,1,130]{3,1,2,0:T(8,128)S(1)}, u32[]{:S(2)}, u32[]{:S(2)}) collective-permute-start(f32[9,8,1,130]{3,1,2,0:T(8,128)S(1)} %get-tuple-element.43), channel_id=1, source_target_pairs={{0,4},{4,8},{8,12},{1,5},{5,9},{9,13},{2,6},{6,10},{10,14},{3,7},{... | collective-permute-start | bytes 112328 | tf_op jit(solution)/shard_map/ppermute | solution.py:21
  15.8 4.9 %collective-permute-start.3 = (f32[9,8,1,130]{3,1,2,0:T(8,128)S(1)}, f32[9,8,1,130]{3,1,2,0:T(8,128)S(1)}, u32[]{:S(2)}, u32[]{:S(2)}) collective-permute-start(f32[9,8,1,130]{3,1,2,0:T(8,128)S(1)} %get-tuple-element.44), channel_id=1, source_target_pairs={{4,0},{8,4},{12,8},{5,1},{9,5},{13,9},{6,2},{10,6},{14,10},{7,3},{... | collective-permute-start | bytes 112328 | tf_op jit(solution)/shard_map/ppermute | solution.py:24
  21.7 7.3 %collective-permute-start.4 = (f32[9,1,18,130]{3,2,1,0:T(8,128)S(1)}, f32[9,1,18,130]{3,2,1,0:T(8,128)S(1)}, u32[]{:S(2)}, u32[]{:S(2)}) collective-permute-start(f32[9,1,18,130]{3,2,1,0:T(8,128)S(1)} %copy.60), channel_id=1, source_target_pairs={{0,1},{1,2},{2,3},{4,5},{5,6},{6,7},{8,9},{9,10},{10,11},{12,13},{... | collective-permute-start | bytes 252728 | tf_op jit(solution)/shard_map/ppermute | solution.py:21
  25.3 8.4 %collective-permute-start.5 = (f32[9,1,18,130]{3,2,1,0:T(8,128)S(1)}, f32[9,1,18,130]{3,2,1,0:T(8,128)S(1)}, u32[]{:S(2)}, u32[]{:S(2)}) collective-permute-start(f32[9,1,18,130]{3,2,1,0:T(8,128)S(1)} %copy.67), channel_id=1, source_target_pairs={{1,0},{2,1},{3,2},{5,4},{6,5},{7,6},{9,8},{10,9},{11,10},{13,12},{... | collective-permute-start | bytes 252728 | tf_op jit(solution)/shard_map/ppermute | solution.py:24
  39.3 1.2 copy-start.3
  40.0 1.8 copy-start.2
  42.8 82.6 %copy-start.5 = (f32[9]{0:T(128)S(1)}, f32[9]{0:T(128)}, u32[]{:S(2)}) copy-start(f32[9]{0:T(128)} %param.11) | copy-start | bytes 112
  216.8 2.0 copy-start.4
